TPU v7x, 16 devices: a whole 2x2x2 slice. The times are simulated.
16 devices in a mesh: data: 16 (over z, y, x, core).
Axes of the slice: x: 2, y: 2, z: 2, core: 2. Of those that a mesh axis runs over, the one named last changes fastest.
Arguments:
- tokens: bfloat16 [16384, 1280], P('data')
- targets: bfloat16 [16384, 1280], P('data')
- w_in: bfloat16 [4, 1280, 5120], replicated
- w_out: bfloat16 [4, 5120, 1280], replicated
Outputs:
- output 1: float32 [4, 1280, 5120], P(None, 'data')
- output 2: float32 [4, 5120, 1280], P(None, 'data')
All inputs are finite; a program needn't handle non-finite values.
Results may differ from a plain program's by a relative error of at most 0.00447066.
Values are sent between devices in bfloat16 or wider.
A program may use at most 1 GiB of HBM per device.

v0:
```python
import jax
import jax.numpy as jnp
from jax import lax
from jax.sharding import PartitionSpec as P


def gelu_act(pre_f32):
    return jax.nn.gelu(pre_f32, approximate=True)


def solution(mesh):
    data_size = mesh.shape["data"]

    def local_grads(tokens, targets, w_in, w_out):
        layers = w_in.shape[0]
        scale = (tokens.shape[0] * data_size) ** -0.5
        hidden = tokens
        saved_fwd = []
        for layer in range(layers):
            pre_act = jnp.dot(hidden, w_in[layer], preferred_element_type=jnp.float32).astype(jnp.bfloat16)
            act_out = gelu_act(pre_act.astype(jnp.float32)).astype(jnp.bfloat16)
            branch = jnp.dot(act_out, w_out[layer], preferred_element_type=jnp.float32)
            saved_fwd.append((hidden, pre_act, act_out))
            hidden = (hidden.astype(jnp.float32) + branch).astype(jnp.bfloat16)
        grad_h = ((hidden.astype(jnp.float32) - targets.astype(jnp.float32)) * scale).astype(jnp.bfloat16)
        shares_first = [None] * layers
        shares_second = [None] * layers
        for layer in reversed(range(layers)):
            hidden_in, pre_act, act_out = saved_fwd[layer]
            grad_second = jnp.einsum("tf,td->fd", act_out, grad_h, preferred_element_type=jnp.float32)
            shares_second[layer] = lax.psum_scatter(grad_second, "data", scatter_dimension=0, tiled=True)
            grad_act = jnp.einsum("td,fd->tf", grad_h, w_out[layer], preferred_element_type=jnp.float32).astype(jnp.bfloat16)
            _, pullback = jax.vjp(gelu_act, pre_act.astype(jnp.float32))
            grad_pre = pullback(grad_act.astype(jnp.float32))[0].astype(jnp.bfloat16)
            grad_first = jnp.einsum("td,tf->df", hidden_in, grad_pre, preferred_element_type=jnp.float32)
            shares_first[layer] = lax.psum_scatter(grad_first, "data", scatter_dimension=0, tiled=True)
            if layer > 0:
                grad_below = jnp.einsum("tf,df->td", grad_pre, w_in[layer], preferred_element_type=jnp.float32)
                grad_h = (grad_h.astype(jnp.float32) + grad_below).astype(jnp.bfloat16)
        return jnp.stack(shares_first), jnp.stack(shares_second)

    tok_spec = P("data", None)
    grad_spec = P(None, "data", None)
    return jax.shard_map(local_grads, mesh=mesh, in_specs=(tok_spec, tok_spec, P(), P()), out_specs=(grad_spec, grad_spec), check_vma=False)
```

profile of v0, /device:TPU:0, one launch (start us, length us, event | category | flops | bytes accessed | tf_op | source)
XLA Modules:
  0.0 2443.4 jit_solution(9300058945757342616)
XLA Ops:
  7.2 21.5 fusion.101
  28.8 24.6 %add_convert_fusion.6 = bf16[1024,1280]{1,0:T(8,128)(2,1)S(1)} fusion(bf16[1024,1280]{1,0:T(8,128)(2,1)S(1)} %copy-done.1, bf16[4,5120,1280]{2,1,0:T(8,128)(2,1)} %param.7, bf16[1024,5120]{1,0:T(8,128)(2,1)} %fusion.101), kind=kOutput, calls=%fused_computation.134 | convolution fusion | flops 13478133760 | bytes 28835840 | tf_op jit(solution)/shard_map/dot_general | solution.py:22
  53.3 22.2 fusion.104
  75.5 24.6 %add_convert_fusion.5 = bf16[1024,1280]{1,0:T(8,128)(2,1)S(1)} fusion(bf16[1024,1280]{1,0:T(8,128)(2,1)S(1)} %add_convert_fusion.6, bf16[4,5120,1280]{2,1,0:T(8,128)(2,1)} %param.7, bf16[1024,5120]{1,0:T(8,128)(2,1)} %fusion.104), kind=kOutput, calls=%fused_computation.133 | convolution fusion | flops 13478133760 | bytes 28835840 | tf_op jit(solution)/shard_map/dot_general | solution.py:22
  100.1 22.2 fusion.107
  122.3 24.6 %add_convert_fusion.4 = bf16[1024,1280]{1,0:T(8,128)(2,1)S(1)} fusion(bf16[1024,1280]{1,0:T(8,128)(2,1)S(1)} %add_convert_fusion.5, bf16[4,5120,1280]{2,1,0:T(8,128)(2,1)} %param.7, bf16[1024,5120]{1,0:T(8,128)(2,1)} %fusion.107), kind=kOutput, calls=%fused_computation.132 | convolution fusion | flops 13478133760 | bytes 28835840 | tf_op jit(solution)/shard_map/dot_general | solution.py:22
  148.4 21.9 fusion.110
  170.3 26.2 %multiply_convert_fusion = bf16[1024,1280]{1,0:T(8,128)(2,1)} fusion(bf16[1024,1280]{1,0:T(8,128)(2,1)S(1)} %copy-done, bf16[4,5120,1280]{2,1,0:T(8,128)(2,1)} %param.7, bf16[1024,1280]{1,0:T(8,128)(2,1)} %copy-done.10, bf16[1024,5120]{1,0:T(8,128)(2,1)} %fusion.110), kind=kOutput, calls=%fused_computation.130 | convolution fusion | flops 13484687360 | bytes 31457280 | tf_op jit(solution)/shard_map/dot_general | solution.py:22
  196.5 28.0 %fusion.6 = bf16[1024,5120]{1,0:T(8,128)(2,1)S(1)} fusion(bf16[1024,5120]{1,0:T(8,128)(2,1)} %fusion.110, bf16[1024,1280]{1,0:T(8,128)(2,1)} %multiply_convert_fusion, bf16[4,5120,1280]{2,1,0:T(8,128)(2,1)} %param.7), kind=kOutput, calls=%fused_computation.31 | convolution fusion | flops 13542359040 | bytes 36700160 | tf_op jit(solution)/shard_map/td,fd->tf/dot_general | solution.py:32
  268.9 27.9 %fusion.9 = bf16[1024,5120]{1,0:T(8,128)(2,1)S(1)} fusion(bf16[1024,5120]{1,0:T(8,128)(2,1)} %fusion.107, bf16[1024,1280]{1,0:T(8,128)(2,1)} %add_convert_fusion.2, bf16[4,5120,1280]{2,1,0:T(8,128)(2,1)} %param.7), kind=kOutput, calls=%fused_computation.34 | convolution fusion | flops 13542359040 | bytes 36700160 | tf_op jit(solution)/shard_map/td,fd->tf/dot_general | solution.py:32
  341.4 28.0 %fusion.12 = bf16[1024,5120]{1,0:T(8,128)(2,1)S(1)} fusion(bf16[1024,5120]{1,0:T(8,128)(2,1)} %fusion.104, bf16[1024,1280]{1,0:T(8,128)(2,1)} %add_convert_fusion.1, bf16[4,5120,1280]{2,1,0:T(8,128)(2,1)} %param.7), kind=kOutput, calls=%fused_computation.37 | convolution fusion | flops 13542359040 | bytes 36700160 | tf_op jit(solution)/shard_map/td,fd->tf/dot_general | solution.py:32
  412.0 42.1 %convolution_bitcast_fusion = f32[1280,5120]{0,1:T(8,128)} fusion(bf16[1024,1280]{1,0:T(8,128)(2,1)S(1)} %copy-done.2, bf16[1024,5120]{1,0:T(8,128)(2,1)} %fusion.101, bf16[1024,1280]{1,0:T(8,128)(2,1)} %add_convert_fusion, bf16[4,5120,1280]{2,1,0:T(8,128)(2,1)} %param.7), kind=kOutput, calls=%fused_computation.28 | convolution fusion | flops 26964131840 | bytes 55050240 | tf_op jit(solution)/shard_map/td,tf->df/dot_general | solution.py:35
  454.1 27.5 %copy.17 = f32[1280,5120]{1,0:T(8,128)} copy(f32[1280,5120]{0,1:T(8,128)} %convolution_bitcast_fusion) | data formatting | bytes 52428800
  483.4 25.0 %fusion.141 = f32[5120,1280]{1,0:T(8,128)} fusion(bf16[1024,1280]{1,0:T(8,128)(2,1)S(1)} %copy-done.13, bf16[1024,5120]{1,0:T(8,128)(2,1)} %fusion.110), kind=kOutput, calls=%fused_computation.141 | convolution fusion | flops 13474201600 | bytes 39321600 | tf_op jit(solution)/shard_map/tf,td->fd/dot_general | solution.py:30
  510.2 25.4 %fusion.144 = f32[5120,1280]{1,0:T(8,128)} fusion(bf16[1024,1280]{1,0:T(8,128)(2,1)S(1)} %copy-done.15, bf16[1024,5120]{1,0:T(8,128)(2,1)} %fusion.107), kind=kOutput, calls=%fused_computation.142 | convolution fusion | flops 13474201600 | bytes 39321600 | tf_op jit(solution)/shard_map/tf,td->fd/dot_general | solution.py:30
  537.3 25.2 %fusion.147 = f32[5120,1280]{1,0:T(8,128)} fusion(bf16[1024,1280]{1,0:T(8,128)(2,1)S(1)} %copy-done.16, bf16[1024,5120]{1,0:T(8,128)(2,1)} %fusion.104), kind=kOutput, calls=%fused_computation.143 | convolution fusion | flops 13474201600 | bytes 39321600 | tf_op jit(solution)/shard_map/tf,td->fd/dot_general | solution.py:30
  564.2 25.2 %fusion.150 = f32[5120,1280]{1,0:T(8,128)} fusion(bf16[1024,1280]{1,0:T(8,128)(2,1)S(1)} %copy-done.17, bf16[1024,5120]{1,0:T(8,128)(2,1)} %fusion.101), kind=kOutput, calls=%fused_computation.144 | convolution fusion | flops 13474201600 | bytes 39321600 | tf_op jit(solution)/shard_map/tf,td->fd/dot_general | solution.py:30
  591.5 202.7 %reduce-scatter.29.cloned.1.call-done = f32[80,5120]{1,0:T(8,128)} async-done(((f32[1280,5120]{1,0:T(8,128)}), f32[80,5120]{1,0:T(8,128)}) %reduce-scatter.29.cloned.1.call-update) | async-done | bytes 1638416
  797.3 269.9 %reduce-scatter.27.cloned.1.call-done = f32[80,5120]{1,0:T(8,128)} async-done(((f32[1280,5120]{1,0:T(8,128)}), f32[80,5120]{1,0:T(8,128)}) %reduce-scatter.27.cloned.1.call-update) | async-done | bytes 1638416
  1070.2 269.8 %reduce-scatter.25.cloned.1.call-done = f32[80,5120]{1,0:T(8,128)} async-done(((f32[1280,5120]{1,0:T(8,128)}), f32[80,5120]{1,0:T(8,128)}) %reduce-scatter.25.cloned.1.call-update) | async-done | bytes 1638416
  1359.8 252.9 %reduce-scatter.23.cloned.1.call-done = f32[320,1280]{1,0:T(8,128)} async-done(((f32[5120,1280]{1,0:T(8,128)}), f32[320,1280]{1,0:T(8,128)}) %reduce-scatter.23.cloned.1.call-update) | async-done | bytes 1638416 | tf_op jit(solution)/shard_map/reduce_scatter | solution.py:31
  1612.7 272.8 %reduce-scatter.21.cloned.1.call-done = f32[320,1280]{1,0:T(8,128)} async-done(((f32[5120,1280]{1,0:T(8,128)}), f32[320,1280]{1,0:T(8,128)}) %reduce-scatter.21.cloned.1.call-update) | async-done | bytes 1638416 | tf_op jit(solution)/shard_map/reduce_scatter | solution.py:31
  1885.5 272.9 %reduce-scatter.19.cloned.1.call-done = f32[320,1280]{1,0:T(8,128)} async-done(((f32[5120,1280]{1,0:T(8,128)}), f32[320,1280]{1,0:T(8,128)}) %reduce-scatter.19.cloned.1.call-update) | async-done | bytes 1638416 | tf_op jit(solution)/shard_map/reduce_scatter | solution.py:31
  2158.4 272.9 %reduce-scatter.17.cloned.1.call-done = f32[320,1280]{1,0:T(8,128)} async-done(((f32[5120,1280]{1,0:T(8,128)}), f32[320,1280]{1,0:T(8,128)}) %reduce-scatter.17.cloned.1.call-update) | async-done | bytes 1638416 | tf_op jit(solution)/shard_map/reduce_scatter | solution.py:31
  (66 shorter events, 172.9 us)
Async XLA Ops:
  7.2 21.6 copy-start.1
  7.2 582.3 %reduce-scatter.31.cloned.1.call-start = ((), (), s32[]{:S(2)}) async-start(), calls=%async_computation.15 | async-start | bytes 27852800
  53.3 22.2 copy-start.6
  100.1 22.2 copy-start.8
  148.4 21.9 copy-start
  196.5 32.0 %copy-start.11 = (bf16[1024,1280]{1,0:T(8,128)(2,1)S(1)}, bf16[1024,1280]{1,0:T(8,128)(2,1)}, u32[]{:S(2)}) copy-start(bf16[1024,1280]{1,0:T(8,128)(2,1)} %copy-done.10) | copy-start | bytes 7864324
  224.6 3.9 copy-start.3
  245.9 1.7 copy-start.12
  245.9 548.3 %reduce-scatter.29.cloned.1.call-start = ((), (), s32[]{:S(2)}) async-start(), calls=%async_computation.14 | async-start | bytes 27852800
  268.9 31.7 %copy-start.9 = (bf16[1024,1280]{1,0:T(8,128)(2,1)S(1)}, bf16[1024,1280]{1,0:T(8,128)(2,1)}, u32[]{:S(2)}) copy-start(bf16[1024,1280]{1,0:T(8,128)(2,1)} %copy-done.8) | copy-start | bytes 7864324
  296.7 3.8 copy-start.4
  318.6 1.7 copy-start.14
  318.6 748.6 %reduce-scatter.27.cloned.1.call-start = ((), (), s32[]{:S(2)}) async-start(), calls=%async_computation.13 | async-start | bytes 27852800
  341.4 31.9 %copy-start.7 = (bf16[1024,1280]{1,0:T(8,128)(2,1)S(1)}, bf16[1024,1280]{1,0:T(8,128)(2,1)}, u32[]{:S(2)}) copy-start(bf16[1024,1280]{1,0:T(8,128)(2,1)} %copy-done.6) | copy-start | bytes 7864324
  369.4 3.9 copy-start.5
  390.8 21.2 copy-start.2
  390.8 949.1 %reduce-scatter.25.cloned.1.call-start = ((), (), s32[]{:S(2)}) async-start(), calls=%async_computation.12 | async-start | bytes 27852800
  481.7 1.7 copy-start.13
  481.7 1131.0 %reduce-scatter.23.cloned.1.call-start = ((), (), s32[]{:S(2)}) async-start(), calls=%async_computation.11 | async-start | bytes 27852800 | tf_op jit(solution)/shard_map/reduce_scatter | solution.py:31
  508.4 1.7 copy-start.15
  508.5 1377.0 %reduce-scatter.21.cloned.1.call-start = ((), (), s32[]{:S(2)}) async-start(), calls=%async_computation.10 | async-start | bytes 27852800 | tf_op jit(solution)/shard_map/reduce_scatter | solution.py:31
  535.6 1.7 copy-start.16
  535.6 1622.8 %reduce-scatter.19.cloned.1.call-start = ((), (), s32[]{:S(2)}) async-start(), calls=%async_computation.9 | async-start | bytes 27852800 | tf_op jit(solution)/shard_map/reduce_scatter | solution.py:31
  562.5 1868.8 %reduce-scatter.17.cloned.1.call-start = ((), (), s32[]{:S(2)}) async-start(), calls=%async_computation.8 | async-start | bytes 27852800 | tf_op jit(solution)/shard_map/reduce_scatter | solution.py:31
  (2 other events, 3.2 us)
Sparse Core Ops, SparseCore 0:
  246.0 275.2 reduce-scatter.30
  523.6 270.6 reduce-scatter.28
  796.5 270.5 reduce-scatter.26
  1069.3 270.6 reduce-scatter.24
  1342.1 270.5 reduce-scatter.22
  1614.8 270.6 reduce-scatter.20
  1887.8 270.5 reduce-scatter.18
  2160.7 270.6 reduce-scatter.16
where the time goes:
time: 2450 us; the launch traced here: 2440 us
  waiting for transfers between devices  1810 us (74%)
  matrix products  531 us (22%)
  local copies, waits for them, and re-layouts  71 us (3%)
    reduce_scatter x4, waiting for transfers between devices, local_grads(): lax.psum_scatter(grad_second, 'data', scatter_dimension=0, tiled=True)  1070 us
    unnamed x12, waiting for transfers between devices  743 us
    dot_general x4, matrix products, local_grads(): jnp.einsum('tf,td->fd', act_out, grad_h, preferred_element_type=jnp.float32)  101 us
    dot_general x4, matrix products, local_grads(): branch = jnp.dot(act_out, w_out[layer], preferred_element_type=jnp.float32)  99.9 us
    dot_general x4, matrix products, local_grads(): jnp.dot(hidden, w_in[layer], preferred_element_type=jnp.float32)  87.9 us
    dot_general x3, matrix products, local_grads(): jnp.einsum('td,fd->tf', grad_h, w_out[layer], preferred_element_type=jnp....  83.9 us
    unnamed x42, local copies, waits for them, and re-layouts  71 us
    dot_general x3, matrix products, local_grads(): jnp.einsum('tf,df->td', grad_pre, w_in[layer], preferred_element_type=jnp...  63.5 us
  transfers between devices with their start and end apart: 8, of which 7 were waited for; matrix products, arithmetic and copies ran while one was open for 14% of the time, Pallas kernels for 0%

commit v1 on v0

v1 whole, which is shorter than its diff:
```python
import functools

import jax
import jax.numpy as jnp
from jax import lax
from jax.experimental import pallas as pl
from jax.experimental.pallas import tpu as pltpu
from jax.sharding import PartitionSpec as P

BF = jnp.bfloat16
F32 = jnp.float32
MESH = pl.DeviceIdType.MESH
VMEM_LIMIT = 67043328

SQRT_2_OVER_PI = 0.7978845608028654
C1 = SQRT_2_OVER_PI * 0.044715


def gelu_parts(x):
    x2 = x * x
    p = C1 * x2 + SQRT_2_OVER_PI
    t = jnp.tanh(x * p)
    s = 0.5 * t + 0.5
    return x2, t, s


def gelu(x):
    _, _, s = gelu_parts(x)
    return x * s


def gelu_grad(x):
    x2, t, s = gelu_parts(x)
    q = (3.0 * C1) * x2 + SQRT_2_OVER_PI
    return s + (0.5 * x) * (1.0 - t * t) * q


def fwd_kernel(scale, chunk, x_ref, t_ref, win_ref, wout_ref, u_ref, at_ref, ht_ref, g_ref, h, acc):
    layer, j = pl.program_id(0), pl.program_id(1)
    last = pl.num_programs(1) - 1
    tokens = h.shape[0]
    sub = ht_ref.shape[1]

    @pl.when((layer == 0) & (j == 0))
    def _():
        h[...] = x_ref[...]

    @pl.when(j == 0)
    def _():
        acc[...] = h[...].astype(F32)

    ht_ref[0] = h[:, pl.ds(pl.multiple_of(j * sub, sub), sub)].T
    for c in range(tokens // chunk):
        rows = slice(c * chunk, (c + 1) * chunk)
        u = jnp.dot(h[rows], win_ref[0], preferred_element_type=F32).astype(BF)
        u_ref[0, rows] = u
        a = gelu(u.astype(F32)).astype(BF)
        at_ref[0, :, rows] = a.T
        acc[rows] += jnp.dot(a, wout_ref[0], preferred_element_type=F32)

    @pl.when(j == last)
    def _():
        h[...] = acc[...].astype(BF)

    @pl.when((j == last) & (layer == pl.num_programs(0) - 1))
    def _():
        g_ref[...] = ((h[...].astype(F32) - t_ref[...].astype(F32)) * scale).astype(BF)


def forward(tokens, targets, w_in, w_out, scale, ftile=512, chunk=512):
    t, d = tokens.shape
    layers, _, ff = w_in.shape
    nj = ff // ftile
    return pl.pallas_call(
        functools.partial(fwd_kernel, scale, chunk),
        grid=(layers, nj),
        in_specs=[
            pl.BlockSpec((t, d), lambda l, j: (0, 0)),
            pl.BlockSpec((t, d), lambda l, j: (0, 0)),
            pl.BlockSpec((1, d, ftile), lambda l, j: (l, 0, j)),
            pl.BlockSpec((1, ftile, d), lambda l, j: (l, j, 0)),
        ],
        out_specs=[
            pl.BlockSpec((1, t, ftile), lambda l, j: (l, 0, j)),
            pl.BlockSpec((1, ftile, t), lambda l, j: (l, j, 0)),
            pl.BlockSpec((1, d // nj, t), lambda l, j: (l, j, 0)),
            pl.BlockSpec((t, d), lambda l, j: (0, 0)),
        ],
        out_shape=[
            jax.ShapeDtypeStruct((layers, t, ff), BF),
            jax.ShapeDtypeStruct((layers, ff, t), BF),
            jax.ShapeDtypeStruct((layers, d, t), BF),
            jax.ShapeDtypeStruct((t, d), BF),
        ],
        scratch_shapes=[pltpu.VMEM((t, d), BF), pltpu.VMEM((t, d), F32)],
        compiler_params=pltpu.CompilerParams(
            dimension_semantics=("arbitrary", "arbitrary"), vmem_limit_bytes=VMEM_LIMIT
        ),
        name="forward",
    )(tokens, targets, w_in, w_out)


ORDERS = ((2, 1, 0), (1, 0, 2), (0, 2, 1))
NIT = 5


def block_index(fixed):
    return tuple(fixed.get(a, slice(None)) for a in range(3))


def bwd_kernel(
    layers, cuts2, cuts1,
    u_hbm, at_hbm, ht_hbm, g_hbm, win_hbm, wout_hbm,
    o1_hbm, o2_hbm,
    g, acc, ht, at, u, wi, wo, v,
    s2, s1, c2, c1, p2, p1, r2a, r2b, r2c, r1a, r1b, r1c,
    sem_g, sem_ht, sem_at, sem_e, sem_out,
    csend, crecv, ssend, srecv, credit,
):
    t, d = g.shape
    ff = u_hbm.shape[2]
    rows2, rows1 = p2.shape[4], p1.shape[4]
    own2 = ff // 16
    fw = ff // NIT
    sub = u.shape[2]
    nsub = fw // sub
    half = t // 2
    total = layers * NIT

    me = lax.axis_index("data")
    bc = lax.rem(me, 2)
    bx = lax.rem(lax.div(me, 2), 2)
    by = lax.rem(lax.div(me, 4), 2)
    bz = lax.div(me, 8)
    bits = (bz, by, bx)
    partner = tuple(me + (1 - 2 * b) * s for b, s in zip(bits, (8, 4, 2)))
    sibling = me + 1 - 2 * bc

    def flip(b, r):
        return 1 - b if r else b

    def owner(rz, ry, rx, rc):
        return 8 * flip(bz, rz) + 4 * flip(by, ry) + 2 * flip(bx, rx) + flip(bc, rc)

    def layer_of(it):
        return layers - 1 - lax.div(it, NIT)

    def at_copies(it):
        slot = lax.rem(it, 2)
        lyr, n = layer_of(it), lax.rem(it, NIT)
        out = []
        for rc in range(2):
            for b in range(8):
                o = owner(b >> 2, (b >> 1) & 1, b & 1, rc)
                row = pl.multiple_of(o * own2 + n * rows2, rows2)
                out.append(pltpu.make_async_copy(
                    at_hbm.at[lyr, pl.ds(row, rows2)], at.at[slot, rc, pl.ds(b * rows2, rows2)], sem_at.at[slot]))
        return out

    def at_wait(it):
        slot = lax.rem(it, 2)
        for rc in range(2):
            pltpu.make_async_copy(at_hbm.at[0, pl.ds(0, 8 * rows2)], at.at[slot, rc], sem_at.at[slot]).wait()

    def ht_copies(lyr, slot):
        out = []
        for rc in range(2):
            for b in range(8):
                o = owner(b >> 2, (b >> 1) & 1, b & 1, rc)
                row = pl.multiple_of(o * rows1, rows1)
                out.append(pltpu.make_async_copy(
                    ht_hbm.at[lyr, pl.ds(row, rows1)], ht.at[slot, rc, pl.ds(b * rows1, rows1)], sem_ht.at[slot]))
        return out

    def ht_wait(slot):
        for rc in range(2):
            pltpu.make_async_copy(ht_hbm.at[0, pl.ds(0, 8 * rows1)], ht.at[slot, rc], sem_ht.at[slot]).wait()

    def e_copies(m):
        slot = lax.rem(m, 2)
        lyr = layer_of(lax.div(m, nsub))
        col = pl.multiple_of(lax.rem(m, NIT * nsub) * sub, sub)
        return [
            pltpu.make_async_copy(u_hbm.at[lyr, :, pl.ds(col, sub)], u.at[slot], sem_e.at[0, slot]),
            pltpu.make_async_copy(wout_hbm.at[lyr, pl.ds(col, sub)], wo.at[slot], sem_e.at[1, slot]),
            pltpu.make_async_copy(win_hbm.at[lyr, :, pl.ds(col, sub)], wi.at[slot], sem_e.at[2, slot]),
        ]

    def start(copies):
        for c in copies:
            c.start()

    tiles = {
        2: dict(k=0, s=s2, c=c2, p=p2, r=(r2a, r2b, r2c), cuts=cuts2),
        1: dict(k=1, s=s1, c=c1, p=p1, r=(r1a, r1b, r1c), cuts=cuts1),
    }

    def core_copy(ti):
        k = ti["k"]
        return pltpu.make_async_remote_copy(
            src_ref=ti["s"], dst_ref=ti["c"], send_sem=csend.at[k], recv_sem=crecv.at[k],
            device_id=(sibling,), device_id_type=MESH)

    def stage_copy(ti, slot, piece, stage):
        order = ORDERS[piece]
        lo, hi = ti["cuts"][piece]
        fixed = {order[i]: 0 for i in range(stage)}
        fixed[order[stage]] = 1
        src = ti["p"].at[(slot,) + block_index(fixed) + (slice(None), slice(lo, hi))]
        r = ti["r"][stage]
        dst = r.at[(slice(None),) * (len(r.shape) - 1) + (slice(lo, hi),)]
        return pltpu.make_async_remote_copy(
            src_ref=src, dst_ref=dst, send_sem=ssend.at[ti["k"], stage, piece], recv_sem=srecv.at[ti["k"], stage, piece],
            device_id=(partner[order[stage]],), device_id_type=MESH)

    def send_stage(ti, slot, stage):
        for piece in range(3):
            stage_copy(ti, slot, piece, stage).start()

    def take_stage(ti, slot, stage):
        for piece in range(3):
            stage_copy(ti, slot, piece, stage).wait()
        for piece in range(3):
            order = ORDERS[piece]
            lo, hi = ti["cuts"][piece]
            idx = (slot,) + block_index({order[i]: 0 for i in range(stage + 1)}) + (slice(None), slice(lo, hi))
            r = ti["r"][stage]
            ti["p"][idx] += r[(slice(None),) * (len(r.shape) - 1) + (slice(lo, hi),)]

    def out_copy(ti, it):
        slot = lax.rem(it, 2)
        lyr, n = layer_of(it), lax.rem(it, NIT)
        src = ti["p"].at[slot, 0, 0, 0]
        if ti["k"] == 0:
            dst = o2_hbm.at[lyr, pl.ds(pl.multiple_of(n * rows2, rows2), rows2)]
        else:
            dst = o1_hbm.at[lyr, :, pl.ds(pl.multiple_of(n * fw, fw), fw)]
        return pltpu.make_async_copy(src, dst, sem_out.at[ti["k"], slot])

    def first_half(ti, it, lhs, rhs):
        @pl.when(it > 0)
        def _():
            core_copy(ti).wait_send()
        ti["s"][...] = jnp.dot(lhs, rhs, preferred_element_type=F32)

        @pl.when(it > 0)
        def _():
            pl.semaphore_wait(credit.at[ti["k"]], 1)
        core_copy(ti).start()

    def second_half(ti, it, lhs, rhs):
        slot = lax.rem(it, 2)

        @pl.when(it > 1)
        def _():
            out_copy(ti, it - 2).wait()
        core_copy(ti).wait_recv()
        rows = ti["p"].shape[4]
        res = jnp.dot(lhs, rhs, preferred_element_type=F32)
        for b in range(8):
            sl = slice(b * rows, (b + 1) * rows)
            ti["p"][slot, b >> 2, (b >> 1) & 1, b & 1] = res[sl] + ti["c"][sl]

        @pl.when(it < total - 1)
        def _():
            pl.semaphore_signal(credit.at[ti["k"]], inc=1, device_id=(sibling,), device_id_type=MESH)
        send_stage(ti, slot, 0)

    def stage(ti, it, k):
        slot = lax.rem(it, 2)
        take_stage(ti, slot, k - 1)
        if k < 3:
            send_stage(ti, slot, k)
        else:
            out_copy(ti, it).start()

    def e_step(m, below):
        slot = lax.rem(m, 2)
        for c in e_copies(m):
            c.wait()
        vslot = lax.rem(lax.div(m, nsub), 2)
        col = lax.rem(m, nsub) * sub
        for c in range(2):
            rows = slice(c * half, (c + 1) * half)
            e = lax.dot_general(g[rows], wo[slot], (((1,), (1,)), ((), ())), preferred_element_type=F32)
            e = e.astype(BF).astype(F32)
            vv = (gelu_grad(u[slot, rows].astype(F32)) * e).astype(BF)
            v[vslot, rows, pl.ds(pl.multiple_of(col, sub), sub)] = vv
            if below:
                acc[rows] += lax.dot_general(vv, wi[slot], (((1,), (1,)), ((), ())), preferred_element_type=F32)

    barrier = pltpu.get_barrier_semaphore()
    for dev in (sibling,) + partner:
        pl.semaphore_signal(barrier, inc=1, device_id=(dev,), device_id_type=MESH)
    pl.semaphore_wait(barrier, 4)

    load_g = pltpu.make_async_copy(g_hbm, g, sem_g)
    load_g.start()
    start(at_copies(0))
    start(e_copies(0))
    start(ht_copies(layers - 1, 0))
    load_g.wait()
    acc[...] = g[...].astype(F32)
    ht_wait(0)

    t2, t1 = tiles[2], tiles[1]

    def body(it, carry):
        lyr, n = layer_of(it), lax.rem(it, NIT)
        lslot = lax.rem(lax.div(it, NIT), 2)
        slot = lax.rem(it, 2)
        live = it < total

        @pl.when(live)
        def _():
            at_wait(it)

            @pl.when(it + 1 < total)
            def _():
                start(at_copies(it + 1))
            first_half(t2, it, at[slot, 1], g[...])

        def run_e(m):
            @pl.when(m + 1 < total * nsub)
            def _():
                start(e_copies(m + 1))

            @pl.when(lyr > 0)
            def _():
                e_step(m, True)

            @pl.when(lyr == 0)
            def _():
                e_step(m, False)

        @pl.when(live)
        def _():
            run_e(it * nsub)

        @pl.when((it >= 2) & (it <= total + 1))
        def _():
            stage(t2, it - 2, 3)

        @pl.when((it >= 1) & (it <= total))
        def _():
            stage(t2, it - 1, 1)

        @pl.when((it >= 2) & (it <= total + 1))
        def _():
            stage(t1, it - 2, 2)

        @pl.when((it >= 1) & (it <= total))
        def _():
            prev = it - 1
            second_half(t1, prev, ht[lax.rem(lax.div(prev, NIT), 2), 0], v[lax.rem(prev, 2)])

        @pl.when(live)
        def _():
            for k in range(1, nsub):
                run_e(it * nsub + k)

            @pl.when((n == 1) & (lyr > 0))
            def _():
                start(ht_copies(lyr - 1, 1 - lslot))

            @pl.when((n == 0) & (it > 0))
            def _():
                ht_wait(lslot)
            first_half(t1, it, ht[lslot, 1], v[slot])

        @pl.when((it >= 2) & (it <= total + 1))
        def _():
            stage(t1, it - 2, 3)

        @pl.when((it >= 1) & (it <= total))
        def _():
            stage(t1, it - 1, 1)

        @pl.when((it >= 1) & (it <= total))
        def _():
            stage(t2, it - 1, 2)

        @pl.when(live)
        def _():
            second_half(t2, it, at[slot, 0], g[...])

            @pl.when((n == NIT - 1) & (lyr > 0))
            def _():
                new = acc[...].astype(BF)
                g[...] = new
                acc[...] = new.astype(F32)

        return carry

    lax.fori_loop(0, total + 2, body, 0)

    for ti in (t2, t1):
        core_copy(ti).wait_send()
        for it in (total - 2, total - 1):
            out_copy(ti, it).wait()


def backward(u, at, ht, g, w_in, w_out, cuts2, cuts1, sub=512):
    layers, t, ff = u.shape
    d = g.shape[1]
    rows2, rows1, fw = ff // 16 // NIT, d // 16, ff // NIT
    any_spec = pl.BlockSpec(memory_space=pl.ANY)
    scratch = [
        pltpu.VMEM((t, d), BF),
        pltpu.VMEM((t, d), F32),
        pltpu.VMEM((2, 2, 8 * rows1, t), BF),
        pltpu.VMEM((2, 2, 8 * rows2, t), BF),
        pltpu.VMEM((2, t, sub), BF),
        pltpu.VMEM((2, d, sub), BF),
        pltpu.VMEM((2, sub, d), BF),
        pltpu.VMEM((2, t, fw), BF),
        pltpu.VMEM((8 * rows2, d), F32),
        pltpu.VMEM((8 * rows1, fw), F32),
        pltpu.VMEM((8 * rows2, d), F32),
        pltpu.VMEM((8 * rows1, fw), F32),
        pltpu.VMEM((2, 2, 2, 2, rows2, d), F32),
        pltpu.VMEM((2, 2, 2, 2, rows1, fw), F32),
        pltpu.VMEM((2, 2, rows2, d), F32),
        pltpu.VMEM((2, rows2, d), F32),
        pltpu.VMEM((rows2, d), F32),
        pltpu.VMEM((2, 2, rows1, fw), F32),
        pltpu.VMEM((2, rows1, fw), F32),
        pltpu.VMEM((rows1, fw), F32),
        pltpu.SemaphoreType.DMA,
        pltpu.SemaphoreType.DMA((2,)),
        pltpu.SemaphoreType.DMA((2,)),
        pltpu.SemaphoreType.DMA((3, 2)),
        pltpu.SemaphoreType.DMA((2, 2)),
        pltpu.SemaphoreType.DMA((2,)),
        pltpu.SemaphoreType.DMA((2,)),
        pltpu.SemaphoreType.DMA((2, 3, 3)),
        pltpu.SemaphoreType.DMA((2, 3, 3)),
        pltpu.SemaphoreType.REGULAR((2,)),
    ]
    return pl.pallas_call(
        functools.partial(bwd_kernel, layers, cuts2, cuts1),
        in_specs=[any_spec] * 6,
        out_specs=[any_spec] * 2,
        out_shape=[
            jax.ShapeDtypeStruct((layers, d // 16, ff), F32),
            jax.ShapeDtypeStruct((layers, ff // 16, d), F32),
        ],
        scratch_shapes=scratch,
        compiler_params=pltpu.CompilerParams(
            collective_id=0, has_side_effects=True, vmem_limit_bytes=VMEM_LIMIT
        ),
        name="backward",
    )(u, at, ht, g, w_in, w_out)


def make(mesh, ftile=512, chunk=512, sub=512, cuts2=((0, 512), (512, 896), (896, 1280)), cuts1=((0, 256), (256, 640), (640, 1024))):
    data_size = mesh.shape["data"]

    def local_grads(tokens, targets, w_in, w_out):
        scale = (tokens.shape[0] * data_size) ** -0.5
        u, at, ht, g = forward(tokens, targets, w_in, w_out, scale, ftile, chunk)
        o1, o2 = backward(u, at, ht, g, w_in, w_out, cuts2, cuts1, sub)
        return o1, o2

    tok_spec = P("data", None)
    grad_spec = P(None, "data", None)
    return jax.shard_map(
        local_grads, mesh=mesh, in_specs=(tok_spec, tok_spec, P(), P()), out_specs=(grad_spec, grad_spec), check_vma=False
    )


SMALL_ARGS = dict(ftile=160, chunk=16, sub=128, cuts2=((0, 128), (128, 192), (192, 256)), cuts1=((0, 64), (64, 160), (160, 256)))


def solution(mesh):
    return make(mesh)
```

time: 2450 us -> 895 us (0.37)
  waiting for transfers between devices: 1810 us -> 0 us
  Pallas kernels: 0 us -> 885 us
  matrix products: 531 us -> 0 us
  local copies, waits for them, and re-layouts: 71 us -> 9.35 us
    reduce_scatter x4 -> x0, waiting for transfers between devices: 1070 us -> none  [local_grads(): lax.psum_scatter(grad_second, 'data', scatter_dimension=0, tiled=True)]
    pallas_call x0 -> x2, Pallas kernels: none -> 885 us  [the longest x1 741 us: backward(): pl.pallas_call(functools.partial(bwd_kernel, layers, cuts2, cuts1), in_sp...]
    unnamed x12 -> x0, waiting for transfers between devices: 743 us -> none
    dot_general x19 -> x0, matrix products: 478 us -> none  [the longest x4 101 us: local_grads(): jnp.einsum('tf,td->fd', act_out, grad_h, preferred_element_type=jnp.float32)]
    unnamed x42 -> x4, local copies, waits for them, and re-layouts: 71 us -> 9.35 us
    unnamed x3 -> x0, matrix products: 52.8 us -> none
  transfers between devices with their start and end apart: 8 -> 0, of which waited for: 7 -> 0; matrix products, arithmetic and copies ran while one was open for 14% -> 0% of each run, Pallas kernels for 0% -> 0%
where the time goes in v1:
time: 895 us
  Pallas kernels  885 us (99%)
  local copies, waits for them, and re-layouts  9.35 us (1%)
    pallas_call x1, Pallas kernels, backward(): pl.pallas_call(functools.partial(bwd_kernel, layers, cuts2, cuts1), in_sp...  741 us
    pallas_call x1, Pallas kernels, forward(): pl.pallas_call(functools.partial(fwd_kernel, scale, chunk), grid=(layers,...  144 us

profile of v1, /device:TPU:0, one launch (start us, length us, event | category | flops | bytes accessed | tf_op | source)
XLA Modules:
  0.0 894.9 jit_solution(17971781276305460473)
XLA Ops:
  0.6 144.0 %forward.1 = (bf16[4,1024,5120]{2,1,0:T(8,128)(2,1)}, bf16[4,5120,1024]{2,1,0:T(8,128)(2,1)}, bf16[4,1280,1024]{2,1,0:T(8,128)(2,1)}, bf16[1024,1280]{1,0:T(8,128)(2,1)}) custom-call(bf16[1024,1280]{1,0:T(8,128)(2,1)} %x_ref.1, bf16[1024,1280]{1,0:T(8,128)(2,1)} %t_ref.1, bf16[4,1280,5120]{2,1,0:T(8,128)(2,1)} %win_hbm.1, bf16[4,5120,1280]{2,1,0:T(8,128)(2,1)} %wout_hbm.1), custom_call_target="tpu_custom_call" | custom-call | tf_op jit(solution)/shard_map/forward/pallas_call | solution.py:74
  144.6 740.9 %backward.1 = (f32[4,80,5120]{2,1,0:T(8,128)}, f32[4,320,1280]{2,1,0:T(8,128)}) custom-call(bf16[4,1024,5120]{2,1,0:T(8,128)(2,1)} %get-tuple-element.6.u_hbm, bf16[4,5120,1024]{2,1,0:T(8,128)(2,1)} %get-tuple-element.7.at_hbm, bf16[4,1280,1024]{2,1,0:T(8,128)(2,1)} %get-tuple-element.8.ht_hbm, bf16[1024,1280]{1,0:T(8,128)(2,1)} %get-tuple-element.9.g_hbm, ...), custom_call_target="tpu_custom_call" | custom-call | tf_op jit(solution)/shard_map/backward/pallas_call | solution.py:440
  885.5 0.0 copy-start
  885.5 6.6 copy.8
  892.1 0.0 copy-done
  892.1 2.8 copy.9
Async XLA Ops:
  885.5 6.6 copy-start
